TPU v7x, 32 devices: a whole 2x2x4 slice. The times are simulated.
32 devices in a mesh: section: 4 (over z), dp: 8 (over y, x, core).
Axes of the slice: x: 2, y: 2, z: 4, core: 2. Of those that a mesh axis runs over, the one named last changes fastest.
Arguments:
- stream: float32 [2, 64, 16, 16, 128], P(None, 'dp'), may hold values from -6 to 6
- cotangent: float32 [2, 64, 16, 16, 128], P(None, 'dp'), may hold values from -6 to 6
- weights: bfloat16 [4, 2304, 128], P('section'), may hold values from -0.09375 to 0.09375
- master: float32 [4, 2304, 128], P('section', 'dp'), may hold values from -0.09375 to 0.09375
- momentum: float32 [4, 2304, 128], P('section', 'dp'), may hold values from -6 to 6
Outputs:
- new_master: float32 [4, 2304, 128], P('section', 'dp')
- new_momentum: float32 [4, 2304, 128], P('section', 'dp')
- new_weights: bfloat16 [4, 2304, 128], P('section')
All inputs are finite; a program needn't handle non-finite values.
Results may differ from a plain program's by a relative error of at most 0.014.
Values may be sent and summed in bfloat16 or wider, within the bound.
A program may use at most 64 MiB of HBM per device.

v0:
```python
import jax
import jax.numpy as jnp
from jax import lax
from jax.sharding import PartitionSpec as P

LAYERS = 1
step_size = 0.1
inertia = 0.9


def columns(field):
    height = field.shape[1]
    breadth = field.shape[2]
    padded = jnp.pad(jax.nn.silu(field).astype(jnp.bfloat16), ((0, 0), (1, 1), (1, 1), (0, 0)))
    shifted = [
        padded[:, row_tap : row_tap + height, col_tap : col_tap + breadth, :]
        for row_tap in range(3)
        for col_tap in range(3)
    ]
    return jnp.concatenate(shifted, axis=3).reshape(-1, 9 * field.shape[3])


def convolve(patches, weight, template):
    return jnp.dot(patches, weight, preferred_element_type=jnp.float32).reshape(template.shape)


def spread(rounded, weight, template):
    height, breadth, channels = (template.shape[1], template.shape[2], template.shape[3])
    spread_cols = lax.dot_general(
        rounded, weight, (((1,), (1,)), ((), ())), preferred_element_type=jnp.float32
    )
    spread_cols = spread_cols.reshape(template.shape[0], height, breadth, 9 * channels)
    padded = jnp.pad(spread_cols, ((0, 0), (1, 1), (1, 1), (0, 0)))
    summed = jnp.zeros(template.shape, jnp.float32)
    for row_tap in range(3):
        for col_tap in range(3):
            tap_index = 3 * row_tap + col_tap
            summed = (
                summed
                + padded[
                    :,
                    2 - row_tap : 2 - row_tap + height,
                    2 - col_tap : 2 - col_tap + breadth,
                    tap_index * channels : (tap_index + 1) * channels,
                ]
            )
    return summed


def weight_grad(patches, rounded):
    return lax.dot_general(
        patches, rounded, (((0,), (0,)), ((), ())), preferred_element_type=jnp.float32
    )


def silu_slope(field):
    logistic = jax.nn.sigmoid(field)
    return logistic * (1.0 + field * (1.0 - logistic))


def coupling_forward(first, second, weight_f, weight_g):
    patch_f = columns(second)
    out_first = first + convolve(patch_f, weight_f, second)
    patch_g = columns(out_first)
    out_second = second + convolve(patch_g, weight_g, out_first)
    return (out_first, out_second, patch_f, patch_g)


def coupling_grads(
    patch_f, second, patch_g, out_first, grad_first, grad_second, weight_f, weight_g
):
    channels = out_first.shape[3]
    round_second = grad_second.astype(jnp.bfloat16).reshape(-1, channels)
    wgrad_g = weight_grad(patch_g, round_second)
    grad_first = grad_first + spread(round_second, weight_g, out_first) * silu_slope(out_first)
    round_first = grad_first.astype(jnp.bfloat16).reshape(-1, channels)
    wgrad_f = weight_grad(patch_f, round_first)
    grad_second = grad_second + spread(round_first, weight_f, second) * silu_slope(second)
    return (grad_first, grad_second, wgrad_f, wgrad_g)


def coupling_backward(out_first, out_second, grad_first, grad_second, weight_f, weight_g):
    patch_g = columns(out_first)
    second = out_second - convolve(patch_g, weight_g, out_first)
    patch_f = columns(second)
    first = out_first - convolve(patch_f, weight_f, second)
    grad_first, grad_second, wgrad_f, wgrad_g = coupling_grads(
        patch_f, second, patch_g, out_first, grad_first, grad_second, weight_f, weight_g
    )
    return (first, second, grad_first, grad_second, wgrad_f, wgrad_g)


def replicated_grads(stream, cotangent, weights):
    section_index = lax.axis_index("section")
    sections = lax.axis_size("section")
    channels = weights.shape[2]
    gathered = lax.all_gather(weights, "section", axis=0, tiled=True)
    all_blocks = gathered.reshape(sections, LAYERS, 2, 9 * channels, channels)
    share = stream.shape[1] // sections
    own = lax.dynamic_slice_in_dim(stream, section_index * share, share, 1)
    seed = lax.dynamic_slice_in_dim(cotangent, section_index * share, share, 1)

    def forward_one(section_idx, pair):
        blocks = lax.dynamic_index_in_dim(all_blocks, section_idx, 0, keepdims=False)
        first, second = pair
        first, second, patch_f, patch_g = coupling_forward(
            first, second, blocks[0, 0], blocks[0, 1]
        )
        return (first, second)

    first, second = lax.fori_loop(0, sections, forward_one, (own[0], own[1]))

    def backward_one(turn, carry):
        out_first, out_second, grad_first, grad_second, grads = carry
        section_idx = sections - 1 - turn
        blocks = lax.dynamic_index_in_dim(all_blocks, section_idx, 0, keepdims=False)
        pieces = []
        for coupling in reversed(range(LAYERS)):
            out_first, out_second, grad_first, grad_second, wgrad_f, wgrad_g = coupling_backward(
                out_first,
                out_second,
                grad_first,
                grad_second,
                blocks[coupling, 0],
                blocks[coupling, 1],
            )
            pieces.append(jnp.stack([wgrad_f, wgrad_g]))
        pieces = pieces[::-1]
        grads = lax.dynamic_update_index_in_dim(grads, jnp.stack(pieces), section_idx, 0)
        return (out_first, out_second, grad_first, grad_second, grads)

    grads_zero = jnp.zeros((sections, LAYERS, 2, 9 * channels, channels), jnp.float32)
    result = lax.fori_loop(0, sections, backward_one, (first, second, seed[0], seed[1], grads_zero))
    return lax.psum_scatter(
        result[4].reshape(-1, channels), ("section", "dp"), scatter_dimension=0, tiled=True
    )


def on_device(stream, cotangent, weights, master, momentum):
    summed = replicated_grads(stream, cotangent, weights)
    images = stream.shape[1] * lax.axis_size("dp")
    gradient = summed / images
    new_momentum = inertia * momentum[0] + gradient
    new_master = master[0] - step_size * new_momentum
    new_weights = lax.all_gather(new_master.astype(jnp.bfloat16), "dp", axis=0, tiled=True)
    return (new_master[None], new_momentum[None], new_weights[None])


def solution(mesh):
    placed = (
        P(None, "dp", None, None, None),
        P(None, "dp", None, None, None),
        P("section", None, None),
        P("section", "dp", None),
        P("section", "dp", None),
    )
    return jax.shard_map(
        on_device,
        mesh=mesh,
        in_specs=placed,
        out_specs=(P("section", "dp", None), P("section", "dp", None), P("section", None, None)),
        check_vma=False,
    )
```

profile of v0, /device:TPU:0, one launch (start us, length us, event | category | flops | bytes accessed | tf_op | source)
XLA Modules:
  0.0 230.6 jit_solution(14302645406688901209)
XLA Ops:
  7.2 0.7 all-gather.2.cloned.1.call-update
  7.9 1.3 dynamic-slice_bitcast_fusion.2
  9.2 53.1 %all-gather.2.cloned.1.call-done = bf16[4,2304,128]{2,1,0:T(8,128)(2,1)} async-done(((bf16[1,2304,128]{2,1,0:T(8,128)(2,1)}), bf16[4,2304,128]{2,1,0:T(8,128)(2,1)}) %all-gather.2.cloned.1.call-update) | async-done | bytes 2359312 | tf_op jit(solution)/shard_map/all_gather | solution.py:97
  62.3 13.1 %while.40 = (s32[]{:T(128)}, f32[2,16,16,128]{3,2,1,0:T(8,128)S(1)}, f32[2,16,16,128]{3,2,1,0:T(8,128)S(1)}, bf16[4,1,2,1152,128]{4,3,2,1,0:T(8,128)(2,1)}, s32[]{:T(128)}) while((s32[]{:T(128)}, f32[2,16,16,128]{3,2,1,0:T(8,128)S(1)}, f32[2,16,16,128]{3,2,1,0:T(8,128)S(1)}, bf16[4,1,2,1152,128]{4,3,2,1,0:T(8,128)(2,1)}, s32[]{:T(128)}) %tuple.101), condition=%wide.region_1.2_spmd, body=%wide.region_0.1_spmd.sunk | while | flops 303104000 | bytes 10551369 | solution.py:111
  62.4 1.1 dynamic-slice_bitcast_fusion.8
  63.7 0.1 constant_dynamic-update-slice_fusion.8
  64.0 0.6 multiply_convert_fusion.7
  65.0 0.5 convolution_add_fusion.3
  65.6 1.1 dynamic-slice_bitcast_fusion.8
  67.0 0.1 constant_dynamic-update-slice_fusion.8
  67.3 0.6 multiply_convert_fusion.7
  68.3 0.5 convolution_add_fusion.3
  68.8 0.1 multiply_convert_fusion.6
  68.9 1.1 dynamic-slice_bitcast_fusion.8
  70.2 0.1 constant_dynamic-update-slice_fusion.8
  70.6 0.6 multiply_convert_fusion.7
  71.6 0.5 convolution_add_fusion.3
  72.1 0.1 multiply_convert_fusion.6
  72.2 1.1 dynamic-slice_bitcast_fusion.8
  73.5 0.1 constant_dynamic-update-slice_fusion.8
  73.8 0.6 multiply_convert_fusion.7
  74.9 0.5 convolution_add_fusion.3
  75.4 2.5 %broadcast_in_dim.23 = f32[4,1,2,1152,128]{4,3,2,1,0:T(8,128)} broadcast(f32[]{:T(128)} %constant.135.clone.1), dimensions={} | broadcast | bytes 4718596 | tf_op jit(solution)/shard_map/broadcast_in_dim | solution.py:132
  77.9 27.0 %while.41 = (s32[]{:T(128)}, f32[2,16,16,128]{3,2,1,0:T(8,128)S(1)}, f32[2,16,16,128]{3,2,1,0:T(8,128)S(1)}, f32[2,16,16,128]{3,2,1,0:T(8,128)S(1)}, f32[2,16,16...) while((s32[]{:T(128)}, ...), condition=%wide.region_3.4_spmd, body=%wide.region_2.3_spmd.sunk | while | flops 909082624 | bytes 29098156 | solution.py:133
  77.9 1.1 dynamic-slice_bitcast_fusion.9
  79.0 0.5 fusion.147
  79.5 0.3 fusion.148
  80.3 0.5 convolution_bitcast_fusion.4
  80.8 0.5 fusion.149
  81.3 0.7 fusion.158
  82.5 0.5 convolution_subtract_fusion.3
  83.0 0.5 convolution_bitcast_fusion.5
  83.5 1.1 fusion.167
  84.7 1.1 dynamic-slice_bitcast_fusion.9
  85.8 0.5 fusion.147
  86.3 0.3 fusion.148
  87.1 0.5 convolution_bitcast_fusion.4
  87.6 0.5 fusion.149
  88.1 0.7 fusion.158
  89.3 0.5 convolution_subtract_fusion.3
  89.8 0.5 convolution_bitcast_fusion.5
  90.3 1.1 fusion.167
  91.4 1.1 dynamic-slice_bitcast_fusion.9
  92.5 0.5 fusion.147
  93.0 0.3 fusion.148
  93.8 0.5 convolution_bitcast_fusion.4
  94.3 0.5 fusion.149
  94.8 0.7 fusion.158
  96.0 0.5 convolution_subtract_fusion.3
  96.5 0.5 convolution_bitcast_fusion.5
  97.0 1.1 fusion.167
  98.2 1.1 dynamic-slice_bitcast_fusion.9
  99.3 0.5 fusion.147
  99.7 0.3 fusion.148
  100.6 0.5 convolution_bitcast_fusion.4
  101.1 0.5 fusion.149
  101.6 0.7 fusion.158
  102.8 0.5 convolution_subtract_fusion.3
  103.3 0.5 convolution_bitcast_fusion.5
  103.8 1.1 fusion.167
  104.9 106.5 %reduce-scatter.2.cloned.1.call-done = f32[288,128]{1,0:T(8,128)} async-done(((f32[9216,128]{1,0:T(8,128)}), f32[288,128]{1,0:T(8,128)}) %reduce-scatter.2.cloned.1.call-update) | async-done | bytes 147472 | tf_op jit(solution)/shard_map/reduce_scatter | solution.py:134
  211.4 1.7 fusion.61
  213.0 9.9 %all_gather.7 = bf16[2304,128]{1,0:T(8,128)(2,1)S(1)} all-gather(bf16[288,128]{1,0:T(8,128)(2,1)S(1)} %get-tuple-element.339), channel_id=1, replica_groups=mesh['section'=4,'dp'=8] {'dp'}, dimensions={0}, use_global_device_ids=true | all-gather | bytes 663552 | tf_op jit(solution)/shard_map/all_gather | solution.py:145
  223.0 0.8 copy.77
  (153 shorter events, 7.1 us)
Async XLA Ops:
  7.2 55.1 %all-gather.2.cloned.1.call-start = ((), (), s32[]{:S(2)}) async-start(), calls=%async_computation.1 | async-start | bytes 2949120 | tf_op jit(solution)/shard_map/all_gather | solution.py:97
  7.9 203.5 %reduce-scatter.2.cloned.1.call-start = ((), (), s32[]{:S(2)}) async-start(), calls=%async_computation.2 | async-start | bytes 4866048 | tf_op jit(solution)/shard_map/reduce_scatter | solution.py:134
  104.9 106.5 %copy-start = (f32[1,288,128]{2,1,0:T(8,128)S(1)}, f32[1,288,128]{2,1,0:T(8,128)}, u32[]{:S(2)}) copy-start(f32[1,288,128]{2,1,0:T(8,128)} %param.12) | copy-start | bytes 442372
  104.9 106.5 %copy-start.1 = (f32[1,288,128]{2,1,0:T(8,128)S(1)}, f32[1,288,128]{2,1,0:T(8,128)}, u32[]{:S(2)}) copy-start(f32[1,288,128]{2,1,0:T(8,128)} %param.13) | copy-start | bytes 442372
Sparse Core Ops, SparseCore 0:
  9.5 52.6 all-gather.1
  105.0 106.2 reduce-scatter.1
where the time goes:
time: 231 us
  waiting for transfers between devices  160 us (69%)
  local copies, waits for them, and re-layouts  20.2 us (9%)
  matrix products  16.9 us (7%)
  between operations  14.1 us (6%)
  blocking collectives  9.93 us (4%)
  other arithmetic  8.27 us (4%)
    reduce_scatter x1, waiting for transfers between devices, replicated_grads(): lax.psum_scatter(result[4].reshape(-1, channels), ('section', 'dp'), scat...  106 us
    all_gather x1, waiting for transfers between devices, replicated_grads(): gathered = lax.all_gather(weights, 'section', axis=0, tiled=True)  53.1 us
    all_gather x1, blocking collectives, on_device(): lax.all_gather(new_master.astype(jnp.bfloat16), 'dp', axis=0, tiled=True)  9.93 us
    dot_general x16, matrix products, convolve(): jnp.dot(patches, weight, preferred_element_type=jnp.float32)  9.05 us
    while x124, local copies, waits for them, and re-layouts  5.82 us
  transfers between devices with their start and end apart: 2, of which 2 were waited for; matrix products, arithmetic and copies ran while one was open for 1% of the time, Pallas kernels for 0%

commit v1 on v0

--- a/solution.py
+++ b/solution.py
@@ -6,6 +6,16 @@
 LAYERS = 1
 step_size = 0.1
 inertia = 0.9
+
+
+def pass_along(block, name, d):
+    devices = lax.axis_size(name)
+    current, blocks = (block, [block])
+    for _ in range(devices - 1):
+        current = lax.ppermute(current, name, [(i, (i + 1) % devices) for i in range(devices)])
+        blocks.insert(0, current)
+    row_of_blocks = jnp.concatenate(blocks, axis=d)
+    return jnp.roll(row_of_blocks, (lax.axis_index(name) + 1) * block.shape[d], axis=d)
 
 
 def columns(field):
@@ -94,7 +104,7 @@
     section_index = lax.axis_index("section")
     sections = lax.axis_size("section")
     channels = weights.shape[2]
-    gathered = lax.all_gather(weights, "section", axis=0, tiled=True)
+    gathered = pass_along(weights, "section", 0)
     all_blocks = gathered.reshape(sections, LAYERS, 2, 9 * channels, channels)
     share = stream.shape[1] // sections
     own = lax.dynamic_slice_in_dim(stream, section_index * share, share, 1)

time: 231 us -> 218 us (0.944)
  waiting for transfers between devices: 160 us -> 151 us
  local copies, waits for them, and re-layouts: 20.2 us -> 13.3 us
  starting transfers between devices: 0.08 us -> 3.15 us
    all_gather x1 -> x0, waiting for transfers between devices: 53.1 us -> none  [replicated_grads(): gathered = lax.all_gather(weights, 'section', axis=0, tiled=True)]
    ppermute x0 -> x3, waiting for transfers between devices: none -> 46 us  [pass_along(): lax.ppermute(current, name, [(i, (i + 1) % devices) for i in range(device...]
    squeeze x4, local copies, waits for them, and re-layouts: 4.44 us -> 0.19 us  [backward_one(): lax.dynamic_index_in_dim(all_blocks, section_idx, 0, keepdims=False)]
    squeeze x4, local copies, waits for them, and re-layouts: 4.44 us -> 0.19 us  [forward_one(): lax.dynamic_index_in_dim(all_blocks, section_idx, 0, keepdims=False)]
    ppermute x0 -> x3, starting transfers between devices: none -> 3.11 us  [pass_along(): lax.ppermute(current, name, [(i, (i + 1) % devices) for i in range(device...]
  transfers between devices with their start and end apart: 2 -> 4, of which waited for: 2 -> 4; matrix products, arithmetic and copies ran while one was open for 1% -> 1% of each run, Pallas kernels for 0% -> 0%
where the time goes in v1:
time: 218 us
  waiting for transfers between devices  151 us (69%)
  matrix products  16.9 us (8%)
  between operations  14.1 us (6%)
  local copies, waits for them, and re-layouts  13.3 us (6%)
  blocking collectives  10.1 us (5%)
  other arithmetic  8.27 us (4%)
  starting transfers between devices  3.15 us (1%)
    reduce_scatter x1, waiting for transfers between devices, replicated_grads(): lax.psum_scatter(result[4].reshape(-1, channels), ('section', 'dp'), scat...  105 us
    ppermute x3, waiting for transfers between devices, pass_along(): lax.ppermute(current, name, [(i, (i + 1) % devices) for i in range(device...  46 us
    all_gather x1, blocking collectives, on_device(): lax.all_gather(new_master.astype(jnp.bfloat16), 'dp', axis=0, tiled=True)  10.1 us
    dot_general x16, matrix products, convolve(): jnp.dot(patches, weight, preferred_element_type=jnp.float32)  9.06 us
    while x124, local copies, waits for them, and re-layouts  5.82 us
    dynamic_update_slice x4, other arithmetic, backward_one(): lax.dynamic_update_index_in_dim(grads, jnp.stack(pieces), section_idx, 0)  4.43 us
  transfers between devices with their start and end apart: 4, of which 4 were waited for; matrix products, arithmetic and copies ran while one was open for 1% of the time, Pallas kernels for 0%

profile of v1, /device:TPU:0, one launch (start us, length us, event | category | flops | bytes accessed | tf_op | source)
XLA Modules:
  0.0 218.2 jit_solution(8864133308226609178)
XLA Ops:
  7.2 3.1 %collective-permute-start = (bf16[1,2304,128]{2,1,0:T(8,128)(2,1)}, bf16[1,2304,128]{2,1,0:T(8,128)(2,1)S(1)}, u32[]{:S(2)}, u32[]{:S(2)}) collective-permute-start(bf16[1,2304,128]{2,1,0:T(8,128)(2,1)} %param.11), channel_id=1, source_target_pairs={{0,8},{8,16},{16,24},{24,0},{1,9},{9,17},{17,25},{25,1},{2,10},{10... | collective-permute-start | bytes 1769480 | tf_op jit(solution)/shard_map/ppermute | solution.py:15
  10.3 15.6 %collective-permute-done = bf16[1,2304,128]{2,1,0:T(8,128)(2,1)S(1)} collective-permute-done((bf16[1,2304,128]{2,1,0:T(8,128)(2,1)}, bf16[1,2304,128]{2,1,0:T(8,128)(2,1)S(1)}, u32[]{:S(2)}, u32[]{:S(2)}) %collective-permute-start) | collective-permute-done | bytes 589856 | tf_op jit(solution)/shard_map/ppermute | solution.py:15
  25.9 16.3 %collective-permute-done.1 = bf16[1,2304,128]{2,1,0:T(8,128)(2,1)S(1)} collective-permute-done((bf16[1,2304,128]{2,1,0:T(8,128)(2,1)S(1)}, bf16[1,2304,128]{2,1,0:T(8,128)(2,1)S(1)}, u32[]{:S(2)}, u32[]{:S(2)}) %collective-permute-start.1) | collective-permute-done | bytes 589856 | tf_op jit(solution)/shard_map/ppermute | solution.py:15
  42.2 1.3 dynamic-slice_bitcast_fusion.2
  43.4 14.2 %collective-permute-done.2 = bf16[1,2304,128]{2,1,0:T(8,128)(2,1)S(1)} collective-permute-done((bf16[1,2304,128]{2,1,0:T(8,128)(2,1)S(1)}, bf16[1,2304,128]{2,1,0:T(8,128)(2,1)S(1)}, u32[]{:S(2)}, u32[]{:S(2)}) %collective-permute-start.2) | collective-permute-done | bytes 589856 | tf_op jit(solution)/shard_map/ppermute | solution.py:15
  57.7 0.1 constant_dynamic-update-slice_fusion.10
  57.7 0.1 constant_dynamic-update-slice_fusion.9
  57.8 0.9 copy-done
  59.1 0.2 constant_dynamic-slice_fusion
  59.3 8.9 %while.40 = (s32[]{:T(128)}, f32[2,16,16,128]{3,2,1,0:T(8,128)S(1)}, f32[2,16,16,128]{3,2,1,0:T(8,128)S(1)}, bf16[4,1,2,1152,128]{4,3,2,1,0:T(8,128)(2,1)S(1)}, s32[]{:T(128)}) while((s32[]{:T(128)}, f32[2,16,16,128]{3,2,1,0:T(8,128)S(1)}, f32[2,16,16,128]{3,2,1,0:T(8,128)S(1)}, bf16[4,1,2,1152,128]{4,3,2,1,0:T(8,128)(2,1)S(1)}, ...), condition=%wide.region_1.2_spmd, body=%wide.region_0.1_spmd.sunk | while | flops 303104000 | bytes 10551369 | solution.py:121
  59.3 0.1 multiply_convert_fusion.6
  59.7 0.1 constant_dynamic-update-slice_fusion.16
  60.0 0.6 multiply_convert_fusion.7
  61.0 0.5 convolution_add_fusion.3
  61.5 0.1 multiply_convert_fusion.6
  61.9 0.1 constant_dynamic-update-slice_fusion.16
  62.2 0.6 multiply_convert_fusion.7
  63.3 0.5 convolution_add_fusion.3
  63.8 0.1 multiply_convert_fusion.6
  64.1 0.1 constant_dynamic-update-slice_fusion.16
  64.4 0.6 multiply_convert_fusion.7
  65.5 0.5 convolution_add_fusion.3
  66.0 0.1 multiply_convert_fusion.6
  66.3 0.1 constant_dynamic-update-slice_fusion.16
  66.7 0.6 multiply_convert_fusion.7
  67.7 0.5 convolution_add_fusion.3
  68.2 2.5 %broadcast_in_dim.23 = f32[4,1,2,1152,128]{4,3,2,1,0:T(8,128)} broadcast(f32[]{:T(128)} %constant.158.clone.1), dimensions={} | broadcast | bytes 4718596 | tf_op jit(solution)/shard_map/broadcast_in_dim | solution.py:142
  70.7 22.8 %while.41 = (s32[]{:T(128)}, f32[2,16,16,128]{3,2,1,0:T(8,128)S(1)}, f32[2,16,16,128]{3,2,1,0:T(8,128)S(1)}, f32[2,16,16,128]{3,2,1,0:T(8,128)S(1)}, f32[2,16,16...) while((s32[]{:T(128)}, ...), condition=%wide.region_3.4_spmd, body=%wide.region_2.3_spmd.sunk | while | flops 909082624 | bytes 29098156 | solution.py:143
  70.8 0.5 fusion.147
  71.3 0.3 fusion.148
  72.1 0.5 convolution_bitcast_fusion.4
  72.6 0.5 fusion.149
  73.1 0.7 fusion.158
  74.3 0.5 convolution_subtract_fusion.3
  74.8 0.5 convolution_bitcast_fusion.5
  75.3 1.1 fusion.167
  76.5 0.5 fusion.147
  77.0 0.3 fusion.148
  77.8 0.5 convolution_bitcast_fusion.4
  78.3 0.5 fusion.149
  78.8 0.7 fusion.158
  80.0 0.5 convolution_subtract_fusion.3
  80.5 0.5 convolution_bitcast_fusion.5
  81.0 1.1 fusion.167
  82.2 0.5 fusion.147
  82.7 0.3 fusion.148
  83.5 0.5 convolution_bitcast_fusion.4
  84.0 0.5 fusion.149
  84.5 0.7 fusion.158
  85.7 0.5 convolution_subtract_fusion.3
  86.2 0.5 convolution_bitcast_fusion.5
  86.7 1.1 fusion.167
  87.9 0.5 fusion.147
  88.3 0.3 fusion.148
  89.2 0.5 convolution_bitcast_fusion.4
  89.7 0.5 fusion.149
  90.2 0.7 fusion.158
  91.4 0.5 convolution_subtract_fusion.3
  91.9 0.5 convolution_bitcast_fusion.5
  92.4 1.1 fusion.167
  93.5 105.2 %reduce-scatter.2.cloned.1.call-done = f32[288,128]{1,0:T(8,128)} async-done(((f32[9216,128]{1,0:T(8,128)}), f32[288,128]{1,0:T(8,128)}) %reduce-scatter.2.cloned.1.call-update) | async-done | bytes 147472 | tf_op jit(solution)/shard_map/reduce_scatter | solution.py:144
  198.7 1.7 fusion.61
  200.4 10.1 %all_gather.3 = bf16[2304,128]{1,0:T(8,128)(2,1)S(1)} all-gather(bf16[288,128]{1,0:T(8,128)(2,1)S(1)} %get-tuple-element.328), channel_id=1, replica_groups=mesh['section'=4,'dp'=8] {'dp'}, dimensions={0}, use_global_device_ids=true | all-gather | bytes 663552 | tf_op jit(solution)/shard_map/all_gather | solution.py:155
  210.5 0.8 copy.82
  (167 shorter events, 7.7 us)
Async XLA Ops:
  7.2 191.6 %reduce-scatter.2.cloned.1.call-start = ((), (), s32[]{:S(2)}) async-start(), calls=%async_computation.1 | async-start | bytes 4866048 | tf_op jit(solution)/shard_map/reduce_scatter | solution.py:144
  7.2 18.7 %collective-permute-start = (bf16[1,2304,128]{2,1,0:T(8,128)(2,1)}, bf16[1,2304,128]{2,1,0:T(8,128)(2,1)S(1)}, u32[]{:S(2)}, u32[]{:S(2)}) collective-permute-start(bf16[1,2304,128]{2,1,0:T(8,128)(2,1)} %param.11), channel_id=1, source_target_pairs={{0,8},{8,16},{16,24},{24,0},{1,9},{9,17},{17,25},{25,1},{2,10},{10... | collective-permute-start | bytes 1769480 | tf_op jit(solution)/shard_map/ppermute | solution.py:15
  25.9 16.3 %collective-permute-start.1 = (bf16[1,2304,128]{2,1,0:T(8,128)(2,1)S(1)}, bf16[1,2304,128]{2,1,0:T(8,128)(2,1)S(1)}, u32[]{:S(2)}, u32[]{:S(2)}) collective-permute-start(bf16[1,2304,128]{2,1,0:T(8,128)(2,1)S(1)} %collective-permute-done), channel_id=1, source_target_pairs={{0,8},{8,16},{16,24},{24,0},{1,9},{9,17},{17,25},{25,1},{2,10},{10... | collective-permute-start | bytes 1769480 | tf_op jit(solution)/shard_map/ppermute | solution.py:15
  42.2 15.4 %collective-permute-start.2 = (bf16[1,2304,128]{2,1,0:T(8,128)(2,1)S(1)}, bf16[1,2304,128]{2,1,0:T(8,128)(2,1)S(1)}, u32[]{:S(2)}, u32[]{:S(2)}) collective-permute-start(bf16[1,2304,128]{2,1,0:T(8,128)(2,1)S(1)} %collective-permute-done.1), channel_id=1, source_target_pairs={{0,8},{8,16},{16,24},{24,0},{1,9},{9,17},{17,25},{25,1},{2,10},{10... | collective-permute-start | bytes 1769480 | tf_op jit(solution)/shard_map/ppermute | solution.py:15
  57.6 1.1 copy-start
  93.5 105.3 %copy-start.1 = (f32[1,288,128]{2,1,0:T(8,128)S(1)}, f32[1,288,128]{2,1,0:T(8,128)}, u32[]{:S(2)}) copy-start(f32[1,288,128]{2,1,0:T(8,128)} %param.12) | copy-start | bytes 442372
  93.5 105.3 %copy-start.2 = (f32[1,288,128]{2,1,0:T(8,128)S(1)}, f32[1,288,128]{2,1,0:T(8,128)}, u32[]{:S(2)}) copy-start(f32[1,288,128]{2,1,0:T(8,128)} %param.13) | copy-start | bytes 442372
Sparse Core Ops, SparseCore 0:
  93.6 105.0 reduce-scatter.1
